TPU v7x, 32 devices: a whole 2x2x4 slice. The times are simulated.
32 devices in a mesh: rows: 4 (over y, x), wide: 8 (over z, core).
Axes of the slice: x: 2, y: 2, z: 4, core: 2. Of those that a mesh axis runs over, the one named last changes fastest.
Arguments:
- tokens: bfloat16 [16, 1024, 1024], P('rows', 'wide'), may hold values from -6 to 6
- segments: int32 [16, 1024], P('rows'), may hold values from 0 to 15, never falling along the last dimension, each value on 1 to 128 neighbouring positions
- w_qkv: bfloat16 [2, 1024, 3072], replicated, may hold values from -0.1875 to 0.1875
- b_qkv: float32 [2, 3072], replicated, may hold values from -3 to 3
- w_out: bfloat16 [2, 1024, 1024], replicated, may hold values from -1 to 1
- b_out: float32 [2, 1024], replicated, may hold values from -3 to 3
- norm_gain: float32 [2, 2, 1024], replicated, may hold values from 0.5 to 1.5
- norm_bias: float32 [2, 2, 1024], replicated, may hold values from -2 to 2
- w_up: bfloat16 [2, 4096, 1024], P(None, 'wide'), may hold values from -0.1875 to 0.1875
- b_up: bfloat16 [2, 4096], P(None, 'wide'), may hold values from -3 to 3
- w_down: bfloat16 [2, 4096, 1024], P(None, 'wide'), may hold values from -0.09375 to 0.09375
- b_down: float32 [2, 1024], replicated, may hold values from -2 to 2
- prefix: bfloat16 [2, 2, 64, 1024], replicated, may hold values from -6 to 6
- cotangent: bfloat16 [16, 1024, 1024], P('rows', 'wide'), may hold values from -6 to 6
Outputs:
- output: bfloat16 [16, 1024, 1024], P('rows', 'wide')
- grad_tokens: float32 [16, 1024, 1024], P('rows', 'wide')
- grad_prefix: float32 [2, 2, 64, 1024], replicated
Inputs may be any that keep to these rules, and one draw needn't show every extreme that they name: `segments`: along each row the pair ids never fall, each pair covers 1 to 128 consecutive positions, and some pair covers exactly 128.
All inputs are finite; a program needn't handle non-finite values.
Results may differ from a plain program's by a relative error of at most 0.02.
Values may be sent and summed in bfloat16 or wider, within the bound.
A program may use at most 320 MiB of HBM per device.

v0:
```python
import math
import jax
import jax.numpy as jnp
from jax import lax
from jax.sharding import PartitionSpec as P

HEADS = 16
PAIR_MAX = 128
LAYERS = 2


def extended(block, sides, width):
    for axis, dim in sides:
        count = lax.axis_size(axis)
        forward = [(i, i + 1) for i in range(count - 1)]
        backward = [(target, source) for source, target in forward]
        low = lax.ppermute(
            lax.slice_in_dim(block, block.shape[dim] - width, None, axis=dim), axis, forward
        )
        high = lax.ppermute(lax.slice_in_dim(block, 0, width, axis=dim), axis, backward)
        block = jnp.concatenate([low, block, high], axis=dim)
    return block


def normalize(values, gain, shift):
    center = values - jnp.mean(values, axis=-1, keepdims=True)
    spread = jnp.mean(center * center, axis=-1, keepdims=True)
    return center * lax.rsqrt(spread + 1e-05) * gain + shift


def gelu_exact(values):
    return jax.nn.gelu(values, approximate=False)


def gelu_back(pre_values, grad_values):
    return jax.vjp(gelu_exact, pre_values)[1](grad_values)[0]


def norm_grad(values, gain, shift, grad_values):
    return jax.vjp(lambda inner: normalize(inner, gain, shift), values)[1](grad_values)[0]


def multiply(left, right):
    return jnp.dot(left, right, preferred_element_type=jnp.float32)


def multiply_back(left, right):
    return lax.dot_general(
        left, right, (((1,), (1,)), ((), ())), preferred_element_type=jnp.float32
    )


def local(
    tokens,
    segments,
    w_qkv,
    b_qkv,
    w_out,
    b_out,
    norm_gain,
    norm_bias,
    w_up,
    b_up,
    w_down,
    b_down,
    prefix,
    cotangent,
):
    seqs_here, tok_here, model_width = tokens.shape
    rows_here = seqs_here * tok_here
    head_count = HEADS
    head_size = model_width // head_count
    score_scale = 1.0 / math.sqrt(head_size)
    rim_rows = PAIR_MAX
    prefix_len = prefix.shape[2]
    position = lax.axis_index("wide") * tok_here
    padded_ids = jnp.pad(segments, ((0, 0), (rim_rows, rim_rows)), constant_values=-1)
    query_ids = lax.dynamic_slice_in_dim(segments, position, tok_here, 1)
    window_ids = lax.dynamic_slice_in_dim(padded_ids, position, tok_here + 2 * rim_rows, 1)
    prefix_mask = jnp.ones((seqs_here, prefix_len, tok_here), dtype=bool)
    visible = jnp.concatenate(
        [prefix_mask, window_ids[:, :, None] == query_ids[:, None, :]], axis=1
    )[:, None]

    def split_heads(values):
        return values.reshape(seqs_here, values.shape[1], head_count, head_size)

    def with_prefix(layer_index, member, window_part):
        fixed_rows = jnp.broadcast_to(
            prefix[layer_index, member][None], (seqs_here, prefix_len, model_width)
        )
        return split_heads(jnp.concatenate([fixed_rows, window_part], axis=1))

    def score_block(queries, key_all):
        scores = (
            jnp.einsum("sqhe,skhe->shkq", queries, key_all, preferred_element_type=jnp.float32)
            * score_scale
        )
        return jnp.where(visible, scores, -1e30)

    hidden = tokens.astype(jnp.float32).reshape(rows_here, model_width)
    stored = []
    for layer_index in range(LAYERS):
        qkv_all = multiply(hidden.astype(jnp.bfloat16), w_qkv[layer_index]) + b_qkv[layer_index]
        qkv_low = qkv_all.astype(jnp.bfloat16).reshape(seqs_here, tok_here, 3 * model_width)
        queries = split_heads(qkv_low[:, :, :model_width])
        window = extended(qkv_low[:, :, model_width:], (("wide", 1),), rim_rows)
        key_all = with_prefix(layer_index, 0, window[:, :, :model_width])
        value_all = with_prefix(layer_index, 1, window[:, :, model_width:])
        scores = score_block(queries, key_all)
        top_score = jnp.max(scores, axis=2, keepdims=True)
        exp_scores = jnp.exp(scores - top_score)
        denominator = jnp.sum(exp_scores, axis=2, keepdims=True)
        probs_low = (exp_scores / denominator).astype(jnp.bfloat16)
        log_total = top_score + jnp.log(denominator)
        context = jnp.einsum(
            "shkq,skhe->sqhe", probs_low, value_all, preferred_element_type=jnp.float32
        )
        context_low = context.astype(jnp.bfloat16).reshape(rows_here, model_width)
        attention = multiply(context_low, w_out[layer_index]) + b_out[layer_index]
        pre_norm = hidden + attention
        normed = normalize(pre_norm, norm_gain[layer_index, 0], norm_bias[layer_index, 0])
        normed_low = normed.astype(jnp.bfloat16)
        up_rows = lax.all_gather(w_up[layer_index], "wide", axis=0, tiled=True)
        down_rows = lax.all_gather(w_down[layer_index], "wide", axis=0, tiled=True)
        bias_rows = lax.all_gather(b_up[layer_index], "wide", axis=0, tiled=True)
        pre_rows = multiply_back(normed_low, up_rows) + bias_rows.astype(jnp.float32)
        ffn_out = multiply(gelu_exact(pre_rows).astype(jnp.bfloat16), down_rows)
        kept_ffn = ()
        second_in = normed + ffn_out + b_down[layer_index]
        stored.append(
            (queries, key_all, value_all, log_total, pre_norm, normed_low, second_in, kept_ffn)
        )
        hidden = normalize(second_in, norm_gain[layer_index, 1], norm_bias[layer_index, 1])
    output = hidden.astype(jnp.bfloat16).reshape(seqs_here, tok_here, model_width)
    grad_hidden = cotangent.astype(jnp.float32).reshape(rows_here, model_width)
    prefix_grads = [None] * LAYERS
    for layer_index in reversed(range(LAYERS)):
        queries, key_all, value_all, log_total, pre_norm, normed_low, second_in, kept_ffn = stored[
            layer_index
        ]
        grad_sum2 = norm_grad(
            second_in, norm_gain[layer_index, 1], norm_bias[layer_index, 1], grad_hidden
        )
        grad_ffn_low = grad_sum2.astype(jnp.bfloat16)
        back_up_rows = lax.all_gather(w_up[layer_index], "wide", axis=0, tiled=True)
        back_down_rows = lax.all_gather(w_down[layer_index], "wide", axis=0, tiled=True)
        back_bias_rows = lax.all_gather(b_up[layer_index], "wide", axis=0, tiled=True)
        back_pre_rows = multiply_back(normed_low, back_up_rows) + back_bias_rows.astype(jnp.float32)
        grad_rows = gelu_back(back_pre_rows, multiply_back(grad_ffn_low, back_down_rows)).astype(
            jnp.bfloat16
        )
        grad_from_ffn = multiply(grad_rows, back_up_rows)
        grad_normed = grad_sum2 + grad_from_ffn
        grad_sum1 = norm_grad(
            pre_norm, norm_gain[layer_index, 0], norm_bias[layer_index, 0], grad_normed
        )
        grad_attn_low = grad_sum1.astype(jnp.bfloat16)
        grad_context = multiply_back(grad_attn_low, w_out[layer_index]).astype(jnp.bfloat16)
        grad_context = split_heads(grad_context.reshape(seqs_here, tok_here, model_width))
        scores = score_block(queries, key_all)
        probs = jnp.exp(scores - log_total)
        probs_low = probs.astype(jnp.bfloat16)
        grad_probs = jnp.einsum(
            "sqhe,skhe->shkq", grad_context, value_all, preferred_element_type=jnp.float32
        )
        row_dot = jnp.sum(probs * grad_probs, axis=2, keepdims=True)
        grad_scores = (probs * (grad_probs - row_dot)).astype(jnp.bfloat16)
        grad_queries = (
            jnp.einsum("shkq,skhe->sqhe", grad_scores, key_all, preferred_element_type=jnp.float32)
            * score_scale
        )
        grad_keys = (
            jnp.einsum("shkq,sqhe->skhe", grad_scores, queries, preferred_element_type=jnp.float32)
            * score_scale
        )
        grad_values = jnp.einsum(
            "shkq,sqhe->skhe", probs_low, grad_context, preferred_element_type=jnp.float32
        )
        key_count = grad_keys.shape[1]
        grad_keys = grad_keys.reshape(seqs_here, key_count, model_width)
        grad_values = grad_values.reshape(seqs_here, key_count, model_width)
        prefix_grads[layer_index] = jnp.stack(
            [
                jnp.sum(grad_keys[:, :prefix_len], axis=0),
                jnp.sum(grad_values[:, :prefix_len], axis=0),
            ],
            axis=0,
        )
        grad_window = jnp.concatenate(
            [grad_keys[:, prefix_len:], grad_values[:, prefix_len:]], axis=2
        )
        grad_kv = grad_window[:, rim_rows : rim_rows + tok_here]
        rim_grads = jnp.concatenate(
            [grad_window[:, :rim_rows], grad_window[:, rim_rows + tok_here :]], axis=1
        )
        returned = extended(rim_grads.astype(jnp.bfloat16), (("wide", 1),), rim_rows).astype(
            rim_grads.dtype
        )
        grad_kv = grad_kv + returned[:, :rim_rows]
        grad_kv = grad_kv + returned[:, 3 * rim_rows :]
        grad_qkv = jnp.concatenate(
            [grad_queries.reshape(seqs_here, tok_here, model_width), grad_kv], axis=2
        )
        grad_qkv = grad_qkv.astype(jnp.bfloat16).reshape(rows_here, 3 * model_width)
        grad_hidden = grad_sum1 + multiply_back(grad_qkv, w_qkv[layer_index])
    grad_prefix = lax.psum(jnp.stack(prefix_grads, axis=0), ("rows", "wide"))
    return (output, grad_hidden.reshape(seqs_here, tok_here, model_width), grad_prefix)


def solution(mesh):
    return jax.shard_map(
        local,
        mesh=mesh,
        in_specs=(
            P("rows", "wide", None),
            P("rows", None),
            P(),
            P(),
            P(),
            P(),
            P(),
            P(),
            P(None, "wide", None),
            P(None, "wide"),
            P(None, "wide", None),
            P(),
            P(),
            P("rows", "wide", None),
        ),
        out_specs=(P("rows", "wide", None), P("rows", "wide", None), P()),
        check_vma=False,
    )
```

profile of v0, /device:TPU:0, one launch (start us, length us, event | category | flops | bytes accessed | tf_op | source)
XLA Modules:
  0.0 841.0 jit_solution(1946470250862313874)
XLA Ops:
  28.2 91.8 %all-gather.1 = bf16[1,4096]{1,0:T(2,128)(2,1)S(1)} all-gather(bf16[1,512]{1,0:T(2,128)(2,1)S(1)} %get-tuple-element.50), channel_id=3, replica_groups=mesh['rows'=4,'wide'=8] {'wide'}, dimensions={1}, use_global_device_ids=true | all-gather | bytes 9216 | tf_op jit(solution)/shard_map/all_gather | solution.py:126
  147.1 10.5 %fusion.193 = (f32[4,16,128]{2,1,0:T(8,128)S(1)}, f32[4,16,448,128]{3,2,1,0:T(8,128)}) fusion(bf16[4,448,16,64]{1,3,2,0:T(8,128)(2,1)} %bitcast.215, bf16[4,128,16,64]{1,3,2,0:T(8,128)(2,1)S(1)} %bitcast.223, pred[4,448,128]{2,1,0:T(8,128)(4,1)S(1)} %concatenate.59), kind=kOutput, calls=%fused_computation.264 | convolution fusion | flops 480763904 | bytes 19660800 | tf_op jit(solution)/shard_map/sqhe,skhe->shkq/dot_general | solution.py:96
  157.6 9.0 %fusion = f32[4,16,128]{2,1,0:T(8,128)S(1)} fusion(f32[4,16,448,128]{3,2,1,0:T(8,128)} %get-tuple-element.52, f32[4,16,128]{2,1,0:T(8,128)S(1)} %get-tuple-element.51), kind=kLoop, calls=%fused_computation.18 | loop fusion | flops 7331840 | bytes 14745600 | tf_op jit(solution)/shard_map/reduce_sum | solution.py:113
  166.7 8.5 %fusion.134 = bf16[4,128,16,64]{1,3,2,0:T(8,128)(2,1)S(1)} fusion(bf16[4,448,16,64]{1,3,2,0:T(8,128)(2,1)S(1)} %bitcast.227, f32[4,16,448,128]{3,2,1,0:T(8,128)} %get-tuple-element.52, f32[4,16,128]{2,1,0:T(8,128)S(1)} %fusion, f32[4,16,128]{2,1,0:T(8,128)S(1)} %get-tuple-element.51), kind=kOutput, calls=%fused_computation.183 | convolution fusion | flops 481296384 | bytes 19464192 | tf_op jit(solution)/shard_map/shkq,skhe->sqhe/dot_general | solution.py:116
  178.0 27.0 %fusion.6 = (f32[512,4096]{1,0:T(8,128)}, f32[512,4096]{1,0:T(8,128)}) fusion(f32[4096]{0:T(1024)S(1)} %bitcast.247, bf16[1,4096,1024]{2,1,0:T(8,128)(2,1)} %all-gather.11.cloned.1.call-done, f32[512,1024]{1,0:T(8,128)S(1)} %get-tuple-element.54, f32[1024]{0:T(1024)} %bitcast.272, f32[1024]{0:T(1024)S(1)} %bitcast.259, f32[512]{0:T(512)S(1)} %fusion.163, ...), kind=kOutput, calls=%fused_computation.26 | convolution fusion | flops 4429709312 | bytes 27291648 | tf_op jit(solution)/shard_map/dot_general | solution.py:48
  205.0 12.3 %fusion.195 = (f32[512]{0:T(512)S(1)}, f32[512,1024]{1,0:T(8,128)S(1)}) fusion(f32[1024]{0:T(1024)S(1)} %bitcast.257, bf16[1,4096,1024]{2,1,0:T(8,128)(2,1)} %all-gather.13.cloned.1.call-done, f32[512,4096]{1,0:T(8,128)} %get-tuple-element.55, f32[512,4096]{1,0:T(8,128)} %get-tuple-element.56, f32[4096]{0:T(1024)S(1)} %bitcast.248, ...), kind=kOutput, calls=%fused_computation.266 | convolution fusion | flops 4307025408 | bytes 29394944 | tf_op jit(solution)/shard_map/dot_general | solution.py:44
  232.2 74.9 %all-gather.4 = bf16[1,4096]{1,0:T(2,128)(2,1)S(1)} all-gather(bf16[1,512]{1,0:T(2,128)(2,1)S(1)} %get-tuple-element.49), channel_id=6, replica_groups=mesh['rows'=4,'wide'=8] {'wide'}, dimensions={1}, use_global_device_ids=true | all-gather | bytes 9216 | tf_op jit(solution)/shard_map/all_gather | solution.py:126
  336.2 10.6 %fusion.196 = (f32[4,16,128]{2,1,0:T(8,128)S(1)}, f32[4,16,448,128]{3,2,1,0:T(8,128)}) fusion(bf16[4,448,16,64]{1,3,2,0:T(8,128)(2,1)} %bitcast.217, bf16[4,128,16,64]{1,3,2,0:T(8,128)(2,1)S(1)} %bitcast.225, pred[4,448,128]{2,1,0:T(8,128)(4,1)S(1)} %concatenate.59), kind=kOutput, calls=%fused_computation.267 | convolution fusion | flops 480763904 | bytes 19660800 | tf_op jit(solution)/shard_map/sqhe,skhe->shkq/dot_general | solution.py:96
  346.8 9.1 %fusion.1 = f32[4,16,128]{2,1,0:T(8,128)S(1)} fusion(f32[4,16,448,128]{3,2,1,0:T(8,128)} %get-tuple-element.60, f32[4,16,128]{2,1,0:T(8,128)S(1)} %get-tuple-element.59), kind=kLoop, calls=%fused_computation.19 | loop fusion | flops 7331840 | bytes 14745600 | tf_op jit(solution)/shard_map/reduce_sum | solution.py:113
  355.9 8.6 %fusion.135 = bf16[4,128,16,64]{1,3,2,0:T(8,128)(2,1)S(1)} fusion(bf16[4,448,16,64]{1,3,2,0:T(8,128)(2,1)S(1)} %bitcast.229, f32[4,16,448,128]{3,2,1,0:T(8,128)} %get-tuple-element.60, f32[4,16,128]{2,1,0:T(8,128)S(1)} %fusion.1, f32[4,16,128]{2,1,0:T(8,128)S(1)} %get-tuple-element.59), kind=kOutput, calls=%fused_computation.184 | convolution fusion | flops 481296384 | bytes 19464192 | tf_op jit(solution)/shard_map/shkq,skhe->sqhe/dot_general | solution.py:116
  367.9 26.7 %fusion.7 = (f32[512,4096]{1,0:T(8,128)}, f32[512,4096]{1,0:T(8,128)}) fusion(f32[4096]{0:T(1024)S(1)} %bitcast.250, bf16[1,4096,1024]{2,1,0:T(8,128)(2,1)} %all-gather.15.cloned.1.call-done, f32[512,1024]{1,0:T(8,128)S(1)} %get-tuple-element.62, f32[1024]{0:T(1024)S(1)} %bitcast.268, f32[1024]{0:T(1024)S(1)} %bitcast.265, f32[512]{0:T(512)S(1)} %fusion.165, ...), kind=kOutput, calls=%fused_computation.27 | convolution fusion | flops 4429709312 | bytes 27291648 | tf_op jit(solution)/shard_map/dot_general | solution.py:48
  394.6 11.0 %fusion.198 = (f32[512]{0:T(512)S(1)}, f32[512,1024]{1,0:T(8,128)S(1)}) fusion(f32[1024]{0:T(1024)S(1)} %bitcast.255, bf16[1,4096,1024]{2,1,0:T(8,128)(2,1)} %all-gather.17.cloned.1.call-done, f32[512,4096]{1,0:T(8,128)} %get-tuple-element.63, f32[512,4096]{1,0:T(8,128)} %get-tuple-element.64, f32[4096]{0:T(1024)S(1)} %bitcast.251, ...), kind=kOutput, calls=%fused_computation.269 | convolution fusion | flops 4307025408 | bytes 29394944 | tf_op jit(solution)/shard_map/dot_general | solution.py:44
  408.8 23.4 %multiply_reduce_fusion.4 = (f32[512]{0:T(512)S(1)}, f32[512,1024]{1,0:T(8,128)}) fusion(f32[512,1024]{1,0:T(8,128)S(1)} %get-tuple-element.62, f32[512]{0:T(512)S(1)} %broadcast_multiply_fusion.3, f32[1024]{0:T(1024)S(1)} %bitcast.267, bf16[1,4096,1024]{2,1,0:T(8,128)(2,1)} %all-gather.15.cloned.1.call-done, f32[512,4096]{1,0:T(8,128)} %get-tuple-element.63, ...), kind=kOutput, calls=%fused_computation.153 | convolution fusion | flops 8625586176 | bytes 39872512 | tf_op jit(solution)/shard_map/dot_general | solution.py:44
  440.4 12.0 %fusion.36 = f32[4,16,64,448]{3,2,1,0:T(8,128)} fusion(bf16[4,128,16,64]{1,3,2,0:T(8,128)(2,1)S(1)} %copy.58, f32[4,16,448,128]{3,2,1,0:T(8,128)} %get-tuple-element.60, f32[4,16,128]{2,1,0:T(8,128)S(1)} %log_add_fusion.1), kind=kOutput, calls=%fused_computation.75 | convolution fusion | flops 477102080 | bytes 23101440 | tf_op jit(solution)/shard_map/shkq,sqhe->skhe/dot_general | solution.py:177
  452.4 10.4 %multiply_reduce_fusion.1 = (f32[4,16,128]{2,1,0:T(8,128)S(1)}, f32[4,16,448,128]{3,2,1,0:T(8,128)}) fusion(f32[4,16,448,128]{3,2,1,0:T(8,128)} %get-tuple-element.60, f32[4,16,128]{2,1,0:T(8,128)S(1)} %log_add_fusion.1, bf16[4,448,16,64]{1,3,2,0:T(8,128)(2,1)S(1)} %bitcast.230, bf16[4,128,16,64]{1,3,2,0:T(8,128)(2,1)S(1)} %copy.58), kind=kOutput, calls=%fused_computation.10 | convolution fusion | flops 480763904 | bytes 34144256 | tf_op jit(solution)/shard_map/sqhe,skhe->shkq/dot_general | solution.py:164
  477.2 10.5 %multiply_convert_fusion.1 = bf16[4,16,448,128]{3,2,1,0:T(8,128)(2,1)S(1)} fusion(f32[4,16,448,128]{3,2,1,0:T(8,128)} %get-tuple-element.70, f32[4,16,448,128]{3,2,1,0:T(8,128)} %get-tuple-element.60, f32[4,16,128]{2,1,0:T(8,128)S(1)} %get-tuple-element.69, f32[4,16,128]{2,1,0:T(8,128)S(1)} %log_add_fusion.1), kind=kLoop, calls=%fused_computation.9 | loop fusion | flops 14680064 | bytes 36765696 | tf_op jit(solution)/shard_map/convert_element_type | solution.py:168
  505.2 8.2 fusion.3
  544.9 23.6 %multiply_reduce_fusion.2 = (f32[512]{0:T(512)S(1)}, f32[512,1024]{1,0:T(8,128)}) fusion(f32[512,1024]{1,0:T(8,128)S(1)} %copy-done.14, f32[512]{0:T(512)S(1)} %copy-done.35, f32[1024]{0:T(1024)S(1)} %bitcast.261, bf16[1,4096,1024]{2,1,0:T(8,128)(2,1)} %all-gather.11.cloned.1.call-done, f32[512,4096]{1,0:T(8,128)} %get-tuple-element.55, ...), kind=kOutput, calls=%fused_computation.148 | convolution fusion | flops 8625586176 | bytes 39872512 | tf_op jit(solution)/shard_map/dot_general | solution.py:44
  576.6 11.8 %fusion.34 = f32[4,16,64,448]{3,2,1,0:T(8,128)} fusion(bf16[4,128,16,64]{1,3,2,0:T(8,128)(2,1)S(1)} %copy.65, f32[4,16,448,128]{3,2,1,0:T(8,128)} %get-tuple-element.52, f32[4,16,128]{2,1,0:T(8,128)S(1)} %log_add_fusion), kind=kOutput, calls=%fused_computation.74 | convolution fusion | flops 477102080 | bytes 23101440 | tf_op jit(solution)/shard_map/shkq,sqhe->skhe/dot_general | solution.py:177
  588.5 10.1 %multiply_reduce_fusion = (f32[4,16,128]{2,1,0:T(8,128)S(1)}, f32[4,16,448,128]{3,2,1,0:T(8,128)}) fusion(f32[4,16,448,128]{3,2,1,0:T(8,128)} %get-tuple-element.52, f32[4,16,128]{2,1,0:T(8,128)S(1)} %log_add_fusion, bf16[4,448,16,64]{1,3,2,0:T(8,128)(2,1)S(1)} %bitcast.228, bf16[4,128,16,64]{1,3,2,0:T(8,128)(2,1)S(1)} %copy.65), kind=kOutput, calls=%fused_computation.7 | convolution fusion | flops 480763904 | bytes 34144256 | tf_op jit(solution)/shard_map/sqhe,skhe->shkq/dot_general | solution.py:164
  612.9 10.7 %multiply_convert_fusion = bf16[4,16,448,128]{3,2,1,0:T(8,128)(2,1)S(1)} fusion(f32[4,16,448,128]{3,2,1,0:T(8,128)} %get-tuple-element.76, f32[4,16,448,128]{3,2,1,0:T(8,128)} %get-tuple-element.52, f32[4,16,128]{2,1,0:T(8,128)S(1)} %get-tuple-element.75, f32[4,16,128]{2,1,0:T(8,128)S(1)} %log_add_fusion), kind=kLoop, calls=%fused_computation.6 | loop fusion | flops 14680064 | bytes 36765696 | tf_op jit(solution)/shard_map/convert_element_type | solution.py:168
  641.0 8.2 fusion.2
  654.1 19.9 %collective-permute-start.6 = (bf16[4,128,2048]{2,1,0:T(8,128)(2,1)}, bf16[4,128,2048]{2,1,0:T(8,128)(2,1)}, u32[]{:S(2)}, u32[]{:S(2)}) collective-permute-start(bf16[4,128,2048]{2,1,0:T(8,128)(2,1)} %get-tuple-element.16), channel_id=1, source_target_pairs={{0,1},{1,2},{2,3},{3,4},{4,5},{5,6},{6,7},{8,9},{9,10},{10,11},{11... | collective-permute-start | bytes 6291464 | tf_op jit(solution)/shard_map/ppermute | solution.py:17
  693.5 125.9 %all-reduce.4.cloned.1.call-done = f32[2,2,64,1024]{2,3,1,0:T(8,128)} async-done(((f32[2,2,64,1024]{2,3,1,0:T(8,128)}), f32[2,2,64,1024]{2,3,1,0:T(8,128)}) %all-reduce.4.cloned.1.call-update) | async-done | bytes 1048592 | tf_op jit(solution)/shard_map/psum | solution.py:207
  (272 shorter events, 250.9 us)
Async XLA Ops:
  7.2 170.8 %all-gather.11.cloned.1.call-start = ((), (), s32[]{:S(2)}) async-start(), calls=%async_computation.1 | async-start | bytes 9437184 | tf_op jit(solution)/shard_map/all_gather | solution.py:124
  10.4 194.5 %all-gather.13.cloned.1.call-start = ((), (), s32[]{:S(2)}) async-start(), calls=%async_computation.2 | async-start | bytes 9437184 | tf_op jit(solution)/shard_map/all_gather | solution.py:125
  12.0 355.8 %all-gather.15.cloned.1.call-start = ((), (), s32[]{:S(2)}) async-start(), calls=%async_computation.3 | async-start | bytes 9437184 | tf_op jit(solution)/shard_map/all_gather | solution.py:124
  18.6 103.1 %copy-start.33 = (s32[4,1024]{1,0:T(4,128)S(1)}, s32[4,1024]{1,0:T(4,128)}, u32[]{:S(2)}) copy-start(s32[4,1024]{1,0:T(4,128)} %param.15) | copy-start | bytes 49156
  18.6 103.4 %copy-start.51 = (f32[2,1024]{1,0:T(2,128)S(1)}, f32[2,1024]{1,0:T(2,128)}, u32[]{:S(2)}) copy-start(f32[2,1024]{1,0:T(2,128)} %param.19) | copy-start | bytes 24580
  18.6 104.0 %copy-start.52 = (f32[2,1024]{1,0:T(2,128)S(1)}, f32[2,1024]{1,0:T(2,128)}, u32[]{:S(2)}) copy-start(f32[2,1024]{1,0:T(2,128)} %param.25) | copy-start | bytes 24580
  18.6 104.6 %copy-start.43 = (f32[2,2,1024]{2,1,0:T(2,128)S(1)}, f32[2,2,1024]{2,1,0:T(2,128)}, u32[]{:S(2)}) copy-start(f32[2,2,1024]{2,1,0:T(2,128)} %param.20) | copy-start | bytes 49156
  18.6 105.2 %copy-start.44 = (f32[2,2,1024]{2,1,0:T(2,128)S(1)}, f32[2,2,1024]{2,1,0:T(2,128)}, u32[]{:S(2)}) copy-start(f32[2,2,1024]{2,1,0:T(2,128)} %param.21) | copy-start | bytes 49156
  20.2 106.2 %collective-permute-start.1 = (bf16[4,128,2048]{2,1,0:T(8,128)(2,1)S(1)}, bf16[4,128,2048]{2,1,0:T(8,128)(2,1)}, u32[]{:S(2)}, u32[]{:S(2)}) collective-permute-start(bf16[4,128,2048]{2,1,0:T(8,128)(2,1)S(1)} %slice.238), channel_id=1, source_target_pairs={{1,0},{2,1},{3,2},{4,3},{5,4},{6,5},{7,6},{9,8},{10,9},{11,10},{12... | collective-permute-start | bytes 6291464 | tf_op jit(solution)/shard_map/ppermute | solution.py:20
  21.5 104.9 %collective-permute-start = (bf16[4,128,2048]{2,1,0:T(8,128)(2,1)S(1)}, bf16[4,128,2048]{2,1,0:T(8,128)(2,1)}, u32[]{:S(2)}, u32[]{:S(2)}) collective-permute-start(bf16[4,128,2048]{2,1,0:T(8,128)(2,1)S(1)} %slice.238), channel_id=1, source_target_pairs={{0,1},{1,2},{2,3},{3,4},{4,5},{5,6},{6,7},{8,9},{9,10},{10,11},{11... | collective-permute-start | bytes 6291464 | tf_op jit(solution)/shard_map/ppermute | solution.py:17
  25.9 368.6 %all-gather.17.cloned.1.call-start = ((), (), s32[]{:S(2)}) async-start(), calls=%async_computation.4 | async-start | bytes 9437184 | tf_op jit(solution)/shard_map/all_gather | solution.py:125
  120.0 84.9 %copy-start.45 = (f32[1,4096]{1,0:T(1,128)}, f32[1,4096]{1,0:T(1,128)S(1)}, u32[]{:S(2)}) copy-start(f32[1,4096]{1,0:T(1,128)S(1)} %convert_element_type.132) | copy-start | bytes 49156
  123.8 81.1 %copy-start.56 = (f32[1,1,1024]{2,1,0:T(1,128)}, f32[1,1,1024]{2,1,0:T(1,128)S(1)}, u32[]{:S(2)}) copy-start(f32[1,1,1024]{2,1,0:T(1,128)S(1)} %get-tuple-element.37) | copy-start | bytes 12292
  123.8 241.5 %copy-start.58 = (f32[1,1,1024]{2,1,0:T(1,128)}, f32[1,1,1024]{2,1,0:T(1,128)S(1)}, u32[]{:S(2)}) copy-start(f32[1,1,1024]{2,1,0:T(1,128)S(1)} %get-tuple-element.36) | copy-start | bytes 12292
  177.5 27.4 %copy-start.13 = (f32[512,1024]{1,0:T(8,128)}, f32[512,1024]{1,0:T(8,128)S(1)}, u32[]{:S(2)}) copy-start(f32[512,1024]{1,0:T(8,128)S(1)} %get-tuple-element.54) | copy-start | bytes 6291460
  217.3 148.0 %copy-start.36 = (f32[512]{0:T(512)}, f32[512]{0:T(512)S(1)}, u32[]{:S(2)}) copy-start(f32[512]{0:T(512)S(1)} %broadcast_multiply_fusion.4) | copy-start | bytes 6148
  217.7 147.6 %copy-start.49 = (f32[512]{0:T(512)}, f32[512]{0:T(512)S(1)}, u32[]{:S(2)}) copy-start(f32[512]{0:T(512)S(1)} %fusion.164) | copy-start | bytes 6148
  226.4 84.6 %collective-permute-start.3 = (bf16[4,128,2048]{2,1,0:T(8,128)(2,1)S(1)}, bf16[4,128,2048]{2,1,0:T(8,128)(2,1)}, u32[]{:S(2)}, u32[]{:S(2)}) collective-permute-start(bf16[4,128,2048]{2,1,0:T(8,128)(2,1)S(1)} %slice.242), channel_id=1, source_target_pairs={{1,0},{2,1},{3,2},{4,3},{5,4},{6,5},{7,6},{9,8},{10,9},{11,10},{12... | collective-permute-start | bytes 6291464 | tf_op jit(solution)/shard_map/ppermute | solution.py:20
  227.7 83.3 %collective-permute-start.2 = (bf16[4,128,2048]{2,1,0:T(8,128)(2,1)S(1)}, bf16[4,128,2048]{2,1,0:T(8,128)(2,1)}, u32[]{:S(2)}, u32[]{:S(2)}) collective-permute-start(bf16[4,128,2048]{2,1,0:T(8,128)(2,1)S(1)} %slice.242), channel_id=1, source_target_pairs={{0,1},{1,2},{2,3},{3,4},{4,5},{5,6},{6,7},{8,9},{9,10},{10,11},{11... | collective-permute-start | bytes 6291464 | tf_op jit(solution)/shard_map/ppermute | solution.py:17
  232.1 587.3 %all-reduce.4.cloned.1.call-start = ((), (), s32[]{:S(2)}) async-start(), calls=%async_computation | async-start | bytes 4194304 | tf_op jit(solution)/shard_map/psum | solution.py:207
  518.4 13.3 %collective-permute-start.4 = (bf16[4,128,2048]{2,1,0:T(8,128)(2,1)}, bf16[4,128,2048]{2,1,0:T(8,128)(2,1)}, u32[]{:S(2)}, u32[]{:S(2)}) collective-permute-start(bf16[4,128,2048]{2,1,0:T(8,128)(2,1)} %get-tuple-element.18), channel_id=1, source_target_pairs={{0,1},{1,2},{2,3},{3,4},{4,5},{5,6},{6,7},{8,9},{9,10},{10,11},{11... | collective-permute-start | bytes 6291464 | tf_op jit(solution)/shard_map/ppermute | solution.py:17
  521.8 9.8 %collective-permute-start.5 = (bf16[4,128,2048]{2,1,0:T(8,128)(2,1)}, bf16[4,128,2048]{2,1,0:T(8,128)(2,1)}, u32[]{:S(2)}, u32[]{:S(2)}) collective-permute-start(bf16[4,128,2048]{2,1,0:T(8,128)(2,1)} %get-tuple-element.19), channel_id=1, source_target_pairs={{1,0},{2,1},{3,2},{4,3},{5,4},{6,5},{7,6},{9,8},{10,9},{11,10},{12... | collective-permute-start | bytes 6291464 | tf_op jit(solution)/shard_map/ppermute | solution.py:20
  654.1 168.4 %collective-permute-start.6 = (bf16[4,128,2048]{2,1,0:T(8,128)(2,1)}, bf16[4,128,2048]{2,1,0:T(8,128)(2,1)}, u32[]{:S(2)}, u32[]{:S(2)}) collective-permute-start(bf16[4,128,2048]{2,1,0:T(8,128)(2,1)} %get-tuple-element.16), channel_id=1, source_target_pairs={{0,1},{1,2},{2,3},{3,4},{4,5},{5,6},{6,7},{8,9},{9,10},{10,11},{11... | collective-permute-start | bytes 6291464 | tf_op jit(solution)/shard_map/ppermute | solution.py:17
  674.0 148.6 %collective-permute-start.7 = (bf16[4,128,2048]{2,1,0:T(8,128)(2,1)}, bf16[4,128,2048]{2,1,0:T(8,128)(2,1)}, u32[]{:S(2)}, u32[]{:S(2)}) collective-permute-start(bf16[4,128,2048]{2,1,0:T(8,128)(2,1)} %get-tuple-element.17), channel_id=1, source_target_pairs={{1,0},{2,1},{3,2},{4,3},{5,4},{6,5},{7,6},{9,8},{10,9},{11,10},{12... | collective-permute-start | bytes 6291464 | tf_op jit(solution)/shard_map/ppermute | solution.py:20
  (59 other events, 551.5 us)
Sparse Core Ops, SparseCore 0:
  10.6 101.7 all-gather.10
  114.6 85.6 all-gather.12
  201.9 97.0 all-gather.14
  301.0 86.1 all-gather.16
  684.2 135.1 all-reduce.3
where the time goes:
time: 847 us; the launch traced here: 841 us
  matrix products  257 us (30%)
  blocking collectives  167 us (20%)
  local copies, waits for them, and re-layouts  137 us (16%)
  waiting for transfers between devices  126 us (15%)
  other arithmetic  101 us (12%)
  starting transfers between devices  37.4 us (4%)
  between operations  15.4 us (2%)
    all_gather x2, blocking collectives, local(): bias_rows = lax.all_gather(b_up[layer_index], 'wide', axis=0, tiled=True)  167 us
    psum x1, waiting for transfers between devices, local(): grad_prefix = lax.psum(jnp.stack(prefix_grads, axis=0), ('rows', 'wide'))  126 us
    dot_general x8, matrix products, multiply(): return jnp.dot(left, right, preferred_element_type=jnp.float32)  86.8 us
    dot_general x6, matrix products, multiply_back(): lax.dot_general(left, right, (((1,), (1,)), ((), ())), preferred_element_...  70.4 us
    unnamed x145, local copies, waits for them, and re-layouts  42.3 us
    ppermute x4, starting transfers between devices, extended(): lax.ppermute(lax.slice_in_dim(block, block.shape[dim] - width, None, axis...  32.1 us
    concatenate x4, local copies, waits for them, and re-layouts, with_prefix(): return split_heads(jnp.concatenate([fixed_rows, window_part], axis=1))  25.2 us
    another operation x4, other arithmetic  24.5 us
  transfers between devices with their start and end apart: 13, of which 1 were waited for; matrix products, arithmetic and copies ran while one was open for 28% of the time, Pallas kernels for 0%

commit v1 on v0

--- a/solution.py
+++ b/solution.py
@@ -204,7 +204,7 @@
         )
         grad_qkv = grad_qkv.astype(jnp.bfloat16).reshape(rows_here, 3 * model_width)
         grad_hidden = grad_sum1 + multiply_back(grad_qkv, w_qkv[layer_index])
-    grad_prefix = lax.psum(jnp.stack(prefix_grads, axis=0), ("rows", "wide"))
+    grad_prefix = jnp.sum(lax.all_gather(jnp.stack(prefix_grads, axis=0), ("rows", "wide")), axis=0)
     return (output, grad_hidden.reshape(seqs_here, tok_here, model_width), grad_prefix)
 
 

time: 847 us -> 871 us (1.028)
  waiting for transfers between devices: 126 us -> 144 us
  other arithmetic: 101 us -> 113 us
    all_gather x0 -> x1, waiting for transfers between devices: none -> 144 us  [local(): lax.all_gather(jnp.stack(prefix_grads, axis=0), ('rows', 'wide'))]
    psum x1 -> x0, waiting for transfers between devices: 126 us -> none  [local(): grad_prefix = lax.psum(jnp.stack(prefix_grads, axis=0), ('rows', 'wide'))]
    reduce_sum x0 -> x1, other arithmetic: none -> 12.8 us  [local(): jnp.sum(lax.all_gather(jnp.stack(prefix_grads, axis=0), ('rows', 'wide'))...]
    unnamed x145 -> x154, local copies, waits for them, and re-layouts: 42.3 us -> 41.9 us
  transfers between devices with their start and end apart: 13 -> 13, of which waited for: 1 -> 1; matrix products, arithmetic and copies ran while one was open for 28% -> 32% of each run, Pallas kernels for 0% -> 0%
where the time goes in v1:
time: 871 us; the launch traced here: 864 us
  matrix products  253 us (29%)
  blocking collectives  167 us (19%)
  waiting for transfers between devices  144 us (17%)
  local copies, waits for them, and re-layouts  142 us (16%)
  other arithmetic  113 us (13%)
  starting transfers between devices  30.5 us (4%)
  between operations  15.5 us (2%)
    all_gather x2, blocking collectives, local(): bias_rows = lax.all_gather(b_up[layer_index], 'wide', axis=0, tiled=True)  167 us
    all_gather x1, waiting for transfers between devices, local(): lax.all_gather(jnp.stack(prefix_grads, axis=0), ('rows', 'wide'))  144 us
    dot_general x8, matrix products, multiply(): return jnp.dot(left, right, preferred_element_type=jnp.float32)  86.9 us
    dot_general x6, matrix products, multiply_back(): lax.dot_general(left, right, (((1,), (1,)), ((), ())), preferred_element_...  67.6 us
    unnamed x154, local copies, waits for them, and re-layouts  41.9 us
    concatenate x4, local copies, waits for them, and re-layouts, with_prefix(): return split_heads(jnp.concatenate([fixed_rows, window_part], axis=1))  25.2 us
    ppermute x4, starting transfers between devices, extended(): lax.ppermute(lax.slice_in_dim(block, block.shape[dim] - width, None, axis...  25.2 us
    another operation x4, other arithmetic  24.7 us
  transfers between devices with their start and end apart: 13, of which 1 were waited for; matrix products, arithmetic and copies ran while one was open for 32% of the time, Pallas kernels for 0%

profile of v1, /device:TPU:0, one launch (start us, length us, event | category | flops | bytes accessed | tf_op | source)
XLA Modules:
  0.0 864.4 jit_solution(14200754540990789418)
XLA Ops:
  28.2 91.8 %all-gather.1 = bf16[1,4096]{1,0:T(2,128)(2,1)S(1)} all-gather(bf16[1,512]{1,0:T(2,128)(2,1)S(1)} %get-tuple-element.47), channel_id=3, replica_groups=mesh['rows'=4,'wide'=8] {'wide'}, dimensions={1}, use_global_device_ids=true | all-gather | bytes 9216 | tf_op jit(solution)/shard_map/all_gather | solution.py:126
  147.1 10.5 %fusion.193 = (f32[4,16,128]{2,1,0:T(8,128)S(1)}, f32[4,16,448,128]{3,2,1,0:T(8,128)}) fusion(bf16[4,448,16,64]{1,3,2,0:T(8,128)(2,1)} %bitcast.216, bf16[4,128,16,64]{1,3,2,0:T(8,128)(2,1)S(1)} %bitcast.225, pred[4,448,128]{2,1,0:T(8,128)(4,1)S(1)} %concatenate.59), kind=kOutput, calls=%fused_computation.264 | convolution fusion | flops 480763904 | bytes 19660800 | tf_op jit(solution)/shard_map/sqhe,skhe->shkq/dot_general | solution.py:96
  157.6 9.0 %fusion = f32[4,16,128]{2,1,0:T(8,128)S(1)} fusion(f32[4,16,448,128]{3,2,1,0:T(8,128)} %get-tuple-element.49, f32[4,16,128]{2,1,0:T(8,128)S(1)} %get-tuple-element.48), kind=kLoop, calls=%fused_computation.18 | loop fusion | flops 7331840 | bytes 14745600 | tf_op jit(solution)/shard_map/reduce_sum | solution.py:113
  166.7 8.5 fusion.134
  178.0 27.0 %fusion.6 = (f32[512,4096]{1,0:T(8,128)}, f32[512,4096]{1,0:T(8,128)}) fusion(f32[4096]{0:T(1024)S(1)} %bitcast.249, bf16[1,4096,1024]{2,1,0:T(8,128)(2,1)} %all-gather.13.cloned.1.call-done, f32[512,1024]{1,0:T(8,128)S(1)} %get-tuple-element.51, f32[1024]{0:T(1024)} %bitcast.274, f32[1024]{0:T(1024)S(1)} %bitcast.261, f32[512]{0:T(512)S(1)} %fusion.163, ...), kind=kOutput, calls=%fused_computation.26 | convolution fusion | flops 4429709312 | bytes 27291648 | tf_op jit(solution)/shard_map/dot_general | solution.py:48
  205.0 12.3 %fusion.195 = (f32[512]{0:T(512)S(1)}, f32[512,1024]{1,0:T(8,128)S(1)}) fusion(f32[1024]{0:T(1024)S(1)} %bitcast.259, bf16[1,4096,1024]{2,1,0:T(8,128)(2,1)} %all-gather.15.cloned.1.call-done, f32[512,4096]{1,0:T(8,128)} %get-tuple-element.52, f32[512,4096]{1,0:T(8,128)} %get-tuple-element.53, f32[4096]{0:T(1024)S(1)} %bitcast.250, ...), kind=kOutput, calls=%fused_computation.266 | convolution fusion | flops 4307025408 | bytes 29394944 | tf_op jit(solution)/shard_map/dot_general | solution.py:44
  232.1 74.9 %all-gather.4 = bf16[1,4096]{1,0:T(2,128)(2,1)S(1)} all-gather(bf16[1,512]{1,0:T(2,128)(2,1)S(1)} %get-tuple-element.46), channel_id=6, replica_groups=mesh['rows'=4,'wide'=8] {'wide'}, dimensions={1}, use_global_device_ids=true | all-gather | bytes 9216 | tf_op jit(solution)/shard_map/all_gather | solution.py:126
  336.3 10.6 %fusion.196 = (f32[4,16,128]{2,1,0:T(8,128)S(1)}, f32[4,16,448,128]{3,2,1,0:T(8,128)}) fusion(bf16[4,448,16,64]{1,3,2,0:T(8,128)(2,1)} %bitcast.218, bf16[4,128,16,64]{1,3,2,0:T(8,128)(2,1)S(1)} %bitcast.227, pred[4,448,128]{2,1,0:T(8,128)(4,1)S(1)} %concatenate.59), kind=kOutput, calls=%fused_computation.267 | convolution fusion | flops 480763904 | bytes 19660800 | tf_op jit(solution)/shard_map/sqhe,skhe->shkq/dot_general | solution.py:96
  346.9 9.1 %fusion.1 = f32[4,16,128]{2,1,0:T(8,128)S(1)} fusion(f32[4,16,448,128]{3,2,1,0:T(8,128)} %get-tuple-element.57, f32[4,16,128]{2,1,0:T(8,128)S(1)} %get-tuple-element.56), kind=kLoop, calls=%fused_computation.19 | loop fusion | flops 7331840 | bytes 14745600 | tf_op jit(solution)/shard_map/reduce_sum | solution.py:113
  356.0 8.6 fusion.135
  368.0 26.7 %fusion.7 = (f32[512,4096]{1,0:T(8,128)}, f32[512,4096]{1,0:T(8,128)}) fusion(f32[4096]{0:T(1024)S(1)} %bitcast.252, bf16[1,4096,1024]{2,1,0:T(8,128)(2,1)} %all-gather.17.cloned.1.call-done, f32[512,1024]{1,0:T(8,128)S(1)} %get-tuple-element.59, f32[1024]{0:T(1024)S(1)} %bitcast.270, f32[1024]{0:T(1024)S(1)} %bitcast.267, f32[512]{0:T(512)S(1)} %fusion.165, ...), kind=kOutput, calls=%fused_computation.27 | convolution fusion | flops 4429709312 | bytes 27291648 | tf_op jit(solution)/shard_map/dot_general | solution.py:48
  394.7 11.0 %fusion.198 = (f32[512]{0:T(512)S(1)}, f32[512,1024]{1,0:T(8,128)S(1)}) fusion(f32[1024]{0:T(1024)S(1)} %bitcast.257, bf16[1,4096,1024]{2,1,0:T(8,128)(2,1)} %all-gather.19.cloned.1.call-done, f32[512,4096]{1,0:T(8,128)} %get-tuple-element.60, f32[512,4096]{1,0:T(8,128)} %get-tuple-element.61, f32[4096]{0:T(1024)S(1)} %bitcast.253, ...), kind=kOutput, calls=%fused_computation.269 | convolution fusion | flops 4307025408 | bytes 29394944 | tf_op jit(solution)/shard_map/dot_general | solution.py:44
  409.0 23.4 %multiply_reduce_fusion.4 = (f32[512]{0:T(512)S(1)}, f32[512,1024]{1,0:T(8,128)}) fusion(f32[512,1024]{1,0:T(8,128)S(1)} %get-tuple-element.59, f32[512]{0:T(512)S(1)} %broadcast_multiply_fusion.3, f32[1024]{0:T(1024)S(1)} %bitcast.269, bf16[1,4096,1024]{2,1,0:T(8,128)(2,1)} %all-gather.17.cloned.1.call-done, f32[512,4096]{1,0:T(8,128)} %get-tuple-element.60, ...), kind=kOutput, calls=%fused_computation.153 | convolution fusion | flops 8625586176 | bytes 39872512 | tf_op jit(solution)/shard_map/dot_general | solution.py:44
  440.5 12.0 %fusion.36 = f32[4,16,64,448]{3,2,1,0:T(8,128)} fusion(bf16[4,128,16,64]{1,3,2,0:T(8,128)(2,1)S(1)} %copy.58, f32[4,16,448,128]{3,2,1,0:T(8,128)} %get-tuple-element.57, f32[4,16,128]{2,1,0:T(8,128)S(1)} %log_add_fusion.1), kind=kOutput, calls=%fused_computation.75 | convolution fusion | flops 477102080 | bytes 23101440 | tf_op jit(solution)/shard_map/shkq,sqhe->skhe/dot_general | solution.py:177
  452.5 10.4 %multiply_reduce_fusion.1 = (f32[4,16,128]{2,1,0:T(8,128)S(1)}, f32[4,16,448,128]{3,2,1,0:T(8,128)}) fusion(f32[4,16,448,128]{3,2,1,0:T(8,128)} %get-tuple-element.57, f32[4,16,128]{2,1,0:T(8,128)S(1)} %log_add_fusion.1, bf16[4,448,16,64]{1,3,2,0:T(8,128)(2,1)S(1)} %bitcast.232, bf16[4,128,16,64]{1,3,2,0:T(8,128)(2,1)S(1)} %copy.58), kind=kOutput, calls=%fused_computation.10 | convolution fusion | flops 480763904 | bytes 34144256 | tf_op jit(solution)/shard_map/sqhe,skhe->shkq/dot_general | solution.py:164
  477.4 10.5 %multiply_convert_fusion.1 = bf16[4,16,448,128]{3,2,1,0:T(8,128)(2,1)S(1)} fusion(f32[4,16,448,128]{3,2,1,0:T(8,128)} %get-tuple-element.67, f32[4,16,448,128]{3,2,1,0:T(8,128)} %get-tuple-element.57, f32[4,16,128]{2,1,0:T(8,128)S(1)} %get-tuple-element.66, f32[4,16,128]{2,1,0:T(8,128)S(1)} %log_add_fusion.1), kind=kLoop, calls=%fused_computation.9 | loop fusion | flops 14680064 | bytes 36765696 | tf_op jit(solution)/shard_map/convert_element_type | solution.py:168
  549.5 23.7 %multiply_reduce_fusion.2 = (f32[512]{0:T(512)S(1)}, f32[512,1024]{1,0:T(8,128)}) fusion(f32[512,1024]{1,0:T(8,128)S(1)} %copy-done.15, f32[512]{0:T(512)S(1)} %copy-done.37, f32[1024]{0:T(1024)S(1)} %bitcast.263, bf16[1,4096,1024]{2,1,0:T(8,128)(2,1)} %all-gather.13.cloned.1.call-done, f32[512,4096]{1,0:T(8,128)} %get-tuple-element.52, ...), kind=kOutput, calls=%fused_computation.148 | convolution fusion | flops 8625586176 | bytes 39872512 | tf_op jit(solution)/shard_map/dot_general | solution.py:44
  581.3 11.8 %fusion.34 = f32[4,16,64,448]{3,2,1,0:T(8,128)} fusion(bf16[4,128,16,64]{1,3,2,0:T(8,128)(2,1)S(1)} %copy.65, f32[4,16,448,128]{3,2,1,0:T(8,128)} %get-tuple-element.49, f32[4,16,128]{2,1,0:T(8,128)S(1)} %log_add_fusion), kind=kOutput, calls=%fused_computation.74 | convolution fusion | flops 477102080 | bytes 23101440 | tf_op jit(solution)/shard_map/shkq,sqhe->skhe/dot_general | solution.py:177
  593.2 10.2 %multiply_reduce_fusion = (f32[4,16,128]{2,1,0:T(8,128)S(1)}, f32[4,16,448,128]{3,2,1,0:T(8,128)}) fusion(f32[4,16,448,128]{3,2,1,0:T(8,128)} %get-tuple-element.49, f32[4,16,128]{2,1,0:T(8,128)S(1)} %log_add_fusion, bf16[4,448,16,64]{1,3,2,0:T(8,128)(2,1)S(1)} %bitcast.230, bf16[4,128,16,64]{1,3,2,0:T(8,128)(2,1)S(1)} %copy.65), kind=kOutput, calls=%fused_computation.7 | convolution fusion | flops 480763904 | bytes 34144256 | tf_op jit(solution)/shard_map/sqhe,skhe->shkq/dot_general | solution.py:164
  605.2 10.7 %multiply_convert_fusion = bf16[4,16,448,128]{3,2,1,0:T(8,128)(2,1)S(1)} fusion(f32[4,16,448,128]{3,2,1,0:T(8,128)} %get-tuple-element.73, f32[4,16,448,128]{3,2,1,0:T(8,128)} %get-tuple-element.49, f32[4,16,128]{2,1,0:T(8,128)S(1)} %get-tuple-element.72, f32[4,16,128]{2,1,0:T(8,128)S(1)} %log_add_fusion), kind=kLoop, calls=%fused_computation.6 | loop fusion | flops 14680064 | bytes 36765696 | tf_op jit(solution)/shard_map/convert_element_type | solution.py:168
  653.5 8.4 fusion.2
  666.8 13.0 %collective-permute-start.6 = (bf16[4,128,2048]{2,1,0:T(8,128)(2,1)}, bf16[4,128,2048]{2,1,0:T(8,128)(2,1)}, u32[]{:S(2)}, u32[]{:S(2)}) collective-permute-start(bf16[4,128,2048]{2,1,0:T(8,128)(2,1)} %get-tuple-element.13), channel_id=1, source_target_pairs={{0,1},{1,2},{2,3},{3,4},{4,5},{5,6},{6,7},{8,9},{9,10},{10,11},{11... | collective-permute-start | bytes 6291464 | tf_op jit(solution)/shard_map/ppermute | solution.py:17
  701.0 143.7 %all-gather.21.cloned.1.call-done = f32[64,2,64,1024]{3,2,1,0:T(8,128)} async-done(((f32[2,2,64,1024]{3,2,1,0:T(8,128)}), f32[64,2,64,1024]{3,2,1,0:T(8,128)}) %all-gather.21.cloned.1.call-update) | async-done | bytes 33554448 | tf_op jit(solution)/shard_map/all_gather | solution.py:207
  844.7 12.8 %reduce_sum.260 = f32[2,2,64,1024]{3,2,1,0:T(8,128)} reduce(f32[32,2,2,64,1024]{4,3,2,1,0:T(8,128)} %bitcast.220, f32[]{:T(128)} %constant.23.clone.1), dimensions={0}, to_apply=%region_26.27 | reduce | flops 8126464 | bytes 34603012 | tf_op jit(solution)/shard_map/reduce_sum | solution.py:207
  (284 shorter events, 258.3 us)
Async XLA Ops:
  7.2 170.7 %all-gather.13.cloned.1.call-start = ((), (), s32[]{:S(2)}) async-start(), calls=%async_computation | async-start | bytes 9437184 | tf_op jit(solution)/shard_map/all_gather | solution.py:124
  10.4 194.5 %all-gather.15.cloned.1.call-start = ((), (), s32[]{:S(2)}) async-start(), calls=%async_computation.1 | async-start | bytes 9437184 | tf_op jit(solution)/shard_map/all_gather | solution.py:125
  12.0 355.9 %all-gather.17.cloned.1.call-start = ((), (), s32[]{:S(2)}) async-start(), calls=%async_computation.2 | async-start | bytes 9437184 | tf_op jit(solution)/shard_map/all_gather | solution.py:124
  18.6 103.1 %copy-start.35 = (s32[4,1024]{1,0:T(4,128)S(1)}, s32[4,1024]{1,0:T(4,128)}, u32[]{:S(2)}) copy-start(s32[4,1024]{1,0:T(4,128)} %param.15) | copy-start | bytes 49156
  18.6 103.4 %copy-start.53 = (f32[2,1024]{1,0:T(2,128)S(1)}, f32[2,1024]{1,0:T(2,128)}, u32[]{:S(2)}) copy-start(f32[2,1024]{1,0:T(2,128)} %param.19) | copy-start | bytes 24580
  18.6 104.0 %copy-start.54 = (f32[2,1024]{1,0:T(2,128)S(1)}, f32[2,1024]{1,0:T(2,128)}, u32[]{:S(2)}) copy-start(f32[2,1024]{1,0:T(2,128)} %param.25) | copy-start | bytes 24580
  18.6 104.6 %copy-start.45 = (f32[2,2,1024]{2,1,0:T(2,128)S(1)}, f32[2,2,1024]{2,1,0:T(2,128)}, u32[]{:S(2)}) copy-start(f32[2,2,1024]{2,1,0:T(2,128)} %param.20) | copy-start | bytes 49156
  18.6 105.2 %copy-start.46 = (f32[2,2,1024]{2,1,0:T(2,128)S(1)}, f32[2,2,1024]{2,1,0:T(2,128)}, u32[]{:S(2)}) copy-start(f32[2,2,1024]{2,1,0:T(2,128)} %param.21) | copy-start | bytes 49156
  20.2 106.2 %collective-permute-start.1 = (bf16[4,128,2048]{2,1,0:T(8,128)(2,1)S(1)}, bf16[4,128,2048]{2,1,0:T(8,128)(2,1)}, u32[]{:S(2)}, u32[]{:S(2)}) collective-permute-start(bf16[4,128,2048]{2,1,0:T(8,128)(2,1)S(1)} %slice.238), channel_id=1, source_target_pairs={{1,0},{2,1},{3,2},{4,3},{5,4},{6,5},{7,6},{9,8},{10,9},{11,10},{12... | collective-permute-start | bytes 6291464 | tf_op jit(solution)/shard_map/ppermute | solution.py:20
  21.5 104.9 %collective-permute-start = (bf16[4,128,2048]{2,1,0:T(8,128)(2,1)S(1)}, bf16[4,128,2048]{2,1,0:T(8,128)(2,1)}, u32[]{:S(2)}, u32[]{:S(2)}) collective-permute-start(bf16[4,128,2048]{2,1,0:T(8,128)(2,1)S(1)} %slice.238), channel_id=1, source_target_pairs={{0,1},{1,2},{2,3},{3,4},{4,5},{5,6},{6,7},{8,9},{9,10},{10,11},{11... | collective-permute-start | bytes 6291464 | tf_op jit(solution)/shard_map/ppermute | solution.py:17
  25.9 368.8 %all-gather.19.cloned.1.call-start = ((), (), s32[]{:S(2)}) async-start(), calls=%async_computation.3 | async-start | bytes 9437184 | tf_op jit(solution)/shard_map/all_gather | solution.py:125
  120.0 84.9 %copy-start.47 = (f32[1,4096]{1,0:T(1,128)}, f32[1,4096]{1,0:T(1,128)S(1)}, u32[]{:S(2)}) copy-start(f32[1,4096]{1,0:T(1,128)S(1)} %convert_element_type.132) | copy-start | bytes 49156
  123.8 81.1 %copy-start.58 = (f32[1,1,1024]{2,1,0:T(1,128)}, f32[1,1,1024]{2,1,0:T(1,128)S(1)}, u32[]{:S(2)}) copy-start(f32[1,1,1024]{2,1,0:T(1,128)S(1)} %get-tuple-element.34) | copy-start | bytes 12292
  123.9 241.6 %copy-start.60 = (f32[1,1,1024]{2,1,0:T(1,128)}, f32[1,1,1024]{2,1,0:T(1,128)S(1)}, u32[]{:S(2)}) copy-start(f32[1,1,1024]{2,1,0:T(1,128)S(1)} %get-tuple-element.33) | copy-start | bytes 12292
  177.5 27.4 %copy-start.14 = (f32[512,1024]{1,0:T(8,128)}, f32[512,1024]{1,0:T(8,128)S(1)}, u32[]{:S(2)}) copy-start(f32[512,1024]{1,0:T(8,128)S(1)} %get-tuple-element.51) | copy-start | bytes 6291460
  217.3 148.2 %copy-start.38 = (f32[512]{0:T(512)}, f32[512]{0:T(512)S(1)}, u32[]{:S(2)}) copy-start(f32[512]{0:T(512)S(1)} %broadcast_multiply_fusion.4) | copy-start | bytes 6148
  217.7 147.8 %copy-start.51 = (f32[512]{0:T(512)}, f32[512]{0:T(512)S(1)}, u32[]{:S(2)}) copy-start(f32[512]{0:T(512)S(1)} %fusion.164) | copy-start | bytes 6148
  226.4 84.6 %collective-permute-start.3 = (bf16[4,128,2048]{2,1,0:T(8,128)(2,1)S(1)}, bf16[4,128,2048]{2,1,0:T(8,128)(2,1)}, u32[]{:S(2)}, u32[]{:S(2)}) collective-permute-start(bf16[4,128,2048]{2,1,0:T(8,128)(2,1)S(1)} %slice.242), channel_id=1, source_target_pairs={{1,0},{2,1},{3,2},{4,3},{5,4},{6,5},{7,6},{9,8},{10,9},{11,10},{12... | collective-permute-start | bytes 6291464 | tf_op jit(solution)/shard_map/ppermute | solution.py:20
  227.7 83.3 %collective-permute-start.2 = (bf16[4,128,2048]{2,1,0:T(8,128)(2,1)S(1)}, bf16[4,128,2048]{2,1,0:T(8,128)(2,1)}, u32[]{:S(2)}, u32[]{:S(2)}) collective-permute-start(bf16[4,128,2048]{2,1,0:T(8,128)(2,1)S(1)} %slice.242), channel_id=1, source_target_pairs={{0,1},{1,2},{2,3},{3,4},{4,5},{5,6},{6,7},{8,9},{9,10},{10,11},{11... | collective-permute-start | bytes 6291464 | tf_op jit(solution)/shard_map/ppermute | solution.py:17
  232.1 612.7 %all-gather.21.cloned.1.call-start = ((), (), s32[]{:S(2)}) async-start(), calls=%async_computation.4 | async-start | bytes 34603008 | tf_op jit(solution)/shard_map/all_gather | solution.py:207
  518.6 18.0 %collective-permute-start.4 = (bf16[4,128,2048]{2,1,0:T(8,128)(2,1)}, bf16[4,128,2048]{2,1,0:T(8,128)(2,1)}, u32[]{:S(2)}, u32[]{:S(2)}) collective-permute-start(bf16[4,128,2048]{2,1,0:T(8,128)(2,1)} %get-tuple-element.15), channel_id=1, source_target_pairs={{0,1},{1,2},{2,3},{3,4},{4,5},{5,6},{6,7},{8,9},{9,10},{10,11},{11... | collective-permute-start | bytes 6291464 | tf_op jit(solution)/shard_map/ppermute | solution.py:17
  522.0 14.6 %collective-permute-start.5 = (bf16[4,128,2048]{2,1,0:T(8,128)(2,1)}, bf16[4,128,2048]{2,1,0:T(8,128)(2,1)}, u32[]{:S(2)}, u32[]{:S(2)}) collective-permute-start(bf16[4,128,2048]{2,1,0:T(8,128)(2,1)} %get-tuple-element.16), channel_id=1, source_target_pairs={{1,0},{2,1},{3,2},{4,3},{5,4},{6,5},{7,6},{9,8},{10,9},{11,10},{12... | collective-permute-start | bytes 6291464 | tf_op jit(solution)/shard_map/ppermute | solution.py:20
  666.8 22.6 %collective-permute-start.6 = (bf16[4,128,2048]{2,1,0:T(8,128)(2,1)}, bf16[4,128,2048]{2,1,0:T(8,128)(2,1)}, u32[]{:S(2)}, u32[]{:S(2)}) collective-permute-start(bf16[4,128,2048]{2,1,0:T(8,128)(2,1)} %get-tuple-element.13), channel_id=1, source_target_pairs={{0,1},{1,2},{2,3},{3,4},{4,5},{5,6},{6,7},{8,9},{9,10},{10,11},{11... | collective-permute-start | bytes 6291464 | tf_op jit(solution)/shard_map/ppermute | solution.py:17
  679.8 9.6 %collective-permute-start.7 = (bf16[4,128,2048]{2,1,0:T(8,128)(2,1)}, bf16[4,128,2048]{2,1,0:T(8,128)(2,1)}, u32[]{:S(2)}, u32[]{:S(2)}) collective-permute-start(bf16[4,128,2048]{2,1,0:T(8,128)(2,1)} %get-tuple-element.14), channel_id=1, source_target_pairs={{1,0},{2,1},{3,2},{4,3},{5,4},{6,5},{7,6},{9,8},{10,9},{11,10},{12... | collective-permute-start | bytes 6291464 | tf_op jit(solution)/shard_map/ppermute | solution.py:20
  (64 other events, 594.3 us)
Sparse Core Ops, SparseCore 0:
  10.6 101.7 all-gather.12
  114.6 85.6 all-gather.14
  201.9 97.0 all-gather.16
  301.0 86.1 all-gather.18
  624.7 219.9 all-gather.20
